TPU v7x, 32 devices: a whole 2x2x4 slice. The times are simulated.
32 devices in a mesh: section: 4 (over y, x), dp: 8 (over z, core).
Axes of the slice: x: 2, y: 2, z: 4, core: 2. Of those that a mesh axis runs over, the one named last changes fastest.
Arguments:
- inputs: bfloat16 [8, 128, 16384], P(None, None, 'dp'), may hold values from -6 to 6
- cotangent: bfloat16 [4, 8, 128, 1024], P('section'), may hold values from -0.5 to 0.5
- norm_gain: bfloat16 [4, 16384], P('section', 'dp'), may hold values from 0.099609375 to 1.8984375
- value_weight: bfloat16 [4, 16384, 1024], P('section', 'dp'), may hold values from -0.046875 to 0.046875
- output_weight: bfloat16 [4, 1024, 16384], P('section', None, 'dp'), may hold values from -0.1875 to 0.1875
- left_old: float32 [4, 16, 1024, 1024], P('section', 'dp'), may hold values from -0.4 to 2.4, as said below
- right_old: float32 [4, 1024, 1024], P('section', 'dp'), may hold values from -0.4 to 2.4, as said below
Outputs:
- section_outputs: bfloat16 [4, 8, 128, 16384], P('section', None, None, 'dp')
- left_stats: float32 [4, 16, 1024, 1024], P('section', 'dp')
- right_stats: float32 [4, 1024, 1024], P('section', 'dp')
Inputs may be any that keep to these rules, and one draw needn't show every extreme that they name: `left_old`: symmetric in its last two dimensions. `right_old`: symmetric in its last two dimensions.
All inputs are finite; a program needn't handle non-finite values.
Results may differ from a plain program's by a relative error of at most 0.015.
Values may be sent and summed in bfloat16 or wider, within the bound.
No kernel may reach another device: no remote copies, remote signals or barrier semaphores. Data moves between devices by JAX's collectives and lax.ppermute only.
A program may use at most 128 MiB of HBM per device.

v0:
```python
import jax
import jax.numpy as jnp
from jax import lax
from jax.sharding import PartitionSpec as P

D = 16384
BLOCK = 1024


def passed_along(value, axis, steps):
    count = lax.axis_size(axis)
    initial, last = (max(0, -steps), min(count, count - steps))
    return lax.ppermute(value, axis, [(source, source + steps) for source in range(initial, last)])


def store_slot(buffer, value, position, active):
    before = lax.dynamic_index_in_dim(buffer, position, 0, keepdims=False)
    chosen = jnp.where(active, value, before)
    return lax.dynamic_update_index_in_dim(buffer, chosen, position, 0)


def on_device(inputs, cotangent, norm_gain, value_weight, output_weight, left_old, right_old):
    sections = lax.axis_size("section")
    dp_count = lax.axis_size("dp")
    section_index = lax.axis_index("section")
    owner_index = lax.axis_index("dp")
    micro_count, batch_rows, col_count = inputs.shape
    width_kv = value_weight.shape[2]
    row_share = batch_rows // dp_count
    gain_row = norm_gain[0].astype(jnp.float32)
    w_value = value_weight[0]
    w_output = output_weight[0]
    cotan_all = cotangent[0]
    tick_count = micro_count + sections - 1

    def apply_layer(hidden_in, cotan_rows):
        floats = hidden_in.astype(jnp.float32)
        scaled_in = (floats * gain_row).astype(jnp.bfloat16)
        squares = jnp.sum(floats * floats, axis=1)
        row_total = lax.psum(squares, "dp")
        inv_rms = lax.rsqrt(row_total / D + 0.25)
        summed = lax.psum_scatter(
            jnp.dot(scaled_in, w_value, preferred_element_type=jnp.float32),
            "dp",
            scatter_dimension=0,
            tiled=True,
        )
        own_scale = lax.dynamic_slice_in_dim(inv_rms, owner_index * row_share, row_share, 0)
        value_own = (own_scale[:, None] * summed).astype(jnp.bfloat16)
        values = lax.all_gather(value_own, "dp", axis=0, tiled=True)
        weighted = (inv_rms[:, None] * cotan_rows.astype(jnp.float32)).astype(jnp.bfloat16)
        result = (floats + jnp.dot(values, w_output, preferred_element_type=jnp.float32)).astype(
            jnp.bfloat16
        )
        return (result, scaled_in, weighted)

    contract_rows = (((0,), (0,)), ((), ()))
    stores = (jnp.zeros((col_count, width_kv), jnp.float32),)
    outputs_init = jnp.zeros((micro_count, batch_rows, col_count), jnp.bfloat16)
    incoming_init = jnp.zeros((batch_rows, col_count), jnp.bfloat16)

    def run_tick(tick_index, state_now):
        incoming, outputs_buf, kept = state_now
        slot_index = tick_index - section_index
        active = (slot_index >= 0) & (slot_index < micro_count)
        position = jnp.clip(slot_index, 0, micro_count - 1)
        entering = lax.dynamic_index_in_dim(
            inputs, jnp.clip(tick_index, 0, micro_count - 1).astype(jnp.int32), 0, keepdims=False
        )
        hidden_in = jnp.where(section_index == 0, entering, incoming)
        cotan_rows = lax.dynamic_index_in_dim(cotan_all, position, 0, keepdims=False)
        result, scaled_in, weighted = apply_layer(hidden_in, cotan_rows)
        outputs_buf = store_slot(outputs_buf, result, position, active)
        update = lax.dot_general(
            scaled_in, weighted, contract_rows, preferred_element_type=jnp.float32
        )
        kept = (kept[0] + jnp.where(active, update, 0.0),)
        incoming = passed_along(result, "section", 1)
        return (incoming, outputs_buf, kept)

    final_state = lax.fori_loop(0, tick_count, run_tick, (incoming_init, outputs_init, stores))
    outputs_buf = final_state[1]
    kept = final_state[2]
    gradient = kept[0]
    grad_half = gradient.astype(jnp.bfloat16)
    blocks = grad_half.reshape(col_count // BLOCK, BLOCK, width_kv)
    left_new = (
        left_old[0]
        + jnp.einsum("bik,bjk->bij", blocks, blocks, preferred_element_type=jnp.float32) / BLOCK
    )
    right_rows = lax.psum_scatter(
        lax.dot_general(
            grad_half, grad_half, contract_rows, preferred_element_type=jnp.float32
        ).astype(jnp.bfloat16),
        "dp",
        scatter_dimension=0,
        tiled=True,
    ).astype(jnp.float32)
    right_new = right_old[0] + right_rows / D
    return (outputs_buf[None], left_new[None], right_new[None])


def solution(mesh):
    placed = (
        P(None, None, "dp"),
        P("section", None, None, None),
        P("section", "dp"),
        P("section", "dp", None),
        P("section", None, "dp"),
        P("section", "dp", None, None),
        P("section", "dp", None),
    )
    return jax.shard_map(
        on_device,
        mesh=mesh,
        in_specs=placed,
        out_specs=(
            P("section", None, None, "dp"),
            P("section", "dp", None, None),
            P("section", "dp", None),
        ),
        check_vma=False,
    )
```

profile of v0, /device:TPU:0, one launch (start us, length us, event | category | flops | bytes accessed | tf_op | source)
XLA Modules:
  0.0 838.5 jit_solution(11864549878178650897)
XLA Ops:
  11.3 770.9 %while.20 = (s32[]{:T(128)}, bf16[128,2048]{1,0:T(8,128)(2,1)S(1)}, bf16[8,128,2048]{2,1,0:T(8,128)(2,1)}, f32[2048,1024]{1,0:T(8,128)}, pred[]{:T(512)}, /*inde...) while((s32[]{:T(128)}, bf16[128,2048]{1,0:T(8,128)(2,1)S(1)}, ...), condition=%wide.region_4.5_spmd.clone, body=%wide.region_0.4_spmd.clone.sunk | while | flops 1621000448 | bytes 36261400 | solution.py:81
  16.4 18.1 %psum.15 = f32[128]{0:T(128)S(1)} all-reduce(f32[128]{0:T(128)S(1)} %get-tuple-element.414), channel_id=1, replica_groups=mesh['section'=4,'dp'=8] {'dp'}, use_global_device_ids=true, to_apply=%region_2.2 | all-reduce | flops 128 | bytes 1024 | tf_op jit(solution)/shard_map/while/body/eval_jaxpr/psum | solution.py:40
  35.7 14.9 %reduce-scatter.5.cloned.1.call-done = f32[16,1024]{1,0:T(8,128)} async-done(((f32[128,1024]{1,0:T(8,128)}), f32[16,1024]{1,0:T(8,128)}) %reduce-scatter.5.cloned.1.call-update) | async-done | bytes 65552 | tf_op jit(solution)/shard_map/while/body/eval_jaxpr/reduce_scatter | solution.py:42
  51.5 14.2 %all_gather.11 = bf16[128,1024]{1,0:T(8,128)(2,1)S(1)} all-gather(bf16[16,1024]{1,0:T(8,128)(2,1)S(1)} %multiply_convert_fusion.2), channel_id=1, replica_groups=mesh['section'=4,'dp'=8] {'dp'}, dimensions={0}, use_global_device_ids=true | all-gather | bytes 294912 | tf_op jit(solution)/shard_map/while/body/eval_jaxpr/all_gather | solution.py:50
  78.6 6.0 collective-permute-done
  89.6 13.6 %psum.15 = f32[128]{0:T(128)S(1)} all-reduce(f32[128]{0:T(128)S(1)} %get-tuple-element.414), channel_id=1, replica_groups=mesh['section'=4,'dp'=8] {'dp'}, use_global_device_ids=true, to_apply=%region_2.2 | all-reduce | flops 128 | bytes 1024 | tf_op jit(solution)/shard_map/while/body/eval_jaxpr/psum | solution.py:40
  104.4 15.9 %reduce-scatter.5.cloned.1.call-done = f32[16,1024]{1,0:T(8,128)} async-done(((f32[128,1024]{1,0:T(8,128)}), f32[16,1024]{1,0:T(8,128)}) %reduce-scatter.5.cloned.1.call-update) | async-done | bytes 65552 | tf_op jit(solution)/shard_map/while/body/eval_jaxpr/reduce_scatter | solution.py:42
  121.2 14.2 %all_gather.11 = bf16[128,1024]{1,0:T(8,128)(2,1)S(1)} all-gather(bf16[16,1024]{1,0:T(8,128)(2,1)S(1)} %multiply_convert_fusion.2), channel_id=1, replica_groups=mesh['section'=4,'dp'=8] {'dp'}, dimensions={0}, use_global_device_ids=true | all-gather | bytes 294912 | tf_op jit(solution)/shard_map/while/body/eval_jaxpr/all_gather | solution.py:50
  142.6 8.2 select_add_fusion.2
  159.3 13.7 %psum.15 = f32[128]{0:T(128)S(1)} all-reduce(f32[128]{0:T(128)S(1)} %get-tuple-element.414), channel_id=1, replica_groups=mesh['section'=4,'dp'=8] {'dp'}, use_global_device_ids=true, to_apply=%region_2.2 | all-reduce | flops 128 | bytes 1024 | tf_op jit(solution)/shard_map/while/body/eval_jaxpr/psum | solution.py:40
  174.2 15.9 %reduce-scatter.5.cloned.1.call-done = f32[16,1024]{1,0:T(8,128)} async-done(((f32[128,1024]{1,0:T(8,128)}), f32[16,1024]{1,0:T(8,128)}) %reduce-scatter.5.cloned.1.call-update) | async-done | bytes 65552 | tf_op jit(solution)/shard_map/while/body/eval_jaxpr/reduce_scatter | solution.py:42
  191.0 14.2 %all_gather.11 = bf16[128,1024]{1,0:T(8,128)(2,1)S(1)} all-gather(bf16[16,1024]{1,0:T(8,128)(2,1)S(1)} %multiply_convert_fusion.2), channel_id=1, replica_groups=mesh['section'=4,'dp'=8] {'dp'}, dimensions={0}, use_global_device_ids=true | all-gather | bytes 294912 | tf_op jit(solution)/shard_map/while/body/eval_jaxpr/all_gather | solution.py:50
  212.4 8.2 select_add_fusion.2
  229.1 13.6 %psum.15 = f32[128]{0:T(128)S(1)} all-reduce(f32[128]{0:T(128)S(1)} %get-tuple-element.414), channel_id=1, replica_groups=mesh['section'=4,'dp'=8] {'dp'}, use_global_device_ids=true, to_apply=%region_2.2 | all-reduce | flops 128 | bytes 1024 | tf_op jit(solution)/shard_map/while/body/eval_jaxpr/psum | solution.py:40
  243.9 15.9 %reduce-scatter.5.cloned.1.call-done = f32[16,1024]{1,0:T(8,128)} async-done(((f32[128,1024]{1,0:T(8,128)}), f32[16,1024]{1,0:T(8,128)}) %reduce-scatter.5.cloned.1.call-update) | async-done | bytes 65552 | tf_op jit(solution)/shard_map/while/body/eval_jaxpr/reduce_scatter | solution.py:42
  260.7 14.2 %all_gather.11 = bf16[128,1024]{1,0:T(8,128)(2,1)S(1)} all-gather(bf16[16,1024]{1,0:T(8,128)(2,1)S(1)} %multiply_convert_fusion.2), channel_id=1, replica_groups=mesh['section'=4,'dp'=8] {'dp'}, dimensions={0}, use_global_device_ids=true | all-gather | bytes 294912 | tf_op jit(solution)/shard_map/while/body/eval_jaxpr/all_gather | solution.py:50
  282.1 8.2 select_add_fusion.2
  298.8 13.6 %psum.15 = f32[128]{0:T(128)S(1)} all-reduce(f32[128]{0:T(128)S(1)} %get-tuple-element.414), channel_id=1, replica_groups=mesh['section'=4,'dp'=8] {'dp'}, use_global_device_ids=true, to_apply=%region_2.2 | all-reduce | flops 128 | bytes 1024 | tf_op jit(solution)/shard_map/while/body/eval_jaxpr/psum | solution.py:40
  313.6 15.8 %reduce-scatter.5.cloned.1.call-done = f32[16,1024]{1,0:T(8,128)} async-done(((f32[128,1024]{1,0:T(8,128)}), f32[16,1024]{1,0:T(8,128)}) %reduce-scatter.5.cloned.1.call-update) | async-done | bytes 65552 | tf_op jit(solution)/shard_map/while/body/eval_jaxpr/reduce_scatter | solution.py:42
  330.4 14.2 %all_gather.11 = bf16[128,1024]{1,0:T(8,128)(2,1)S(1)} all-gather(bf16[16,1024]{1,0:T(8,128)(2,1)S(1)} %multiply_convert_fusion.2), channel_id=1, replica_groups=mesh['section'=4,'dp'=8] {'dp'}, dimensions={0}, use_global_device_ids=true | all-gather | bytes 294912 | tf_op jit(solution)/shard_map/while/body/eval_jaxpr/all_gather | solution.py:50
  351.9 8.2 select_add_fusion.2
  368.6 13.7 %psum.15 = f32[128]{0:T(128)S(1)} all-reduce(f32[128]{0:T(128)S(1)} %get-tuple-element.414), channel_id=1, replica_groups=mesh['section'=4,'dp'=8] {'dp'}, use_global_device_ids=true, to_apply=%region_2.2 | all-reduce | flops 128 | bytes 1024 | tf_op jit(solution)/shard_map/while/body/eval_jaxpr/psum | solution.py:40
  383.5 15.9 %reduce-scatter.5.cloned.1.call-done = f32[16,1024]{1,0:T(8,128)} async-done(((f32[128,1024]{1,0:T(8,128)}), f32[16,1024]{1,0:T(8,128)}) %reduce-scatter.5.cloned.1.call-update) | async-done | bytes 65552 | tf_op jit(solution)/shard_map/while/body/eval_jaxpr/reduce_scatter | solution.py:42
  400.3 14.2 %all_gather.11 = bf16[128,1024]{1,0:T(8,128)(2,1)S(1)} all-gather(bf16[16,1024]{1,0:T(8,128)(2,1)S(1)} %multiply_convert_fusion.2), channel_id=1, replica_groups=mesh['section'=4,'dp'=8] {'dp'}, dimensions={0}, use_global_device_ids=true | all-gather | bytes 294912 | tf_op jit(solution)/shard_map/while/body/eval_jaxpr/all_gather | solution.py:50
  421.8 8.2 select_add_fusion.2
  438.5 13.7 %psum.15 = f32[128]{0:T(128)S(1)} all-reduce(f32[128]{0:T(128)S(1)} %get-tuple-element.414), channel_id=1, replica_groups=mesh['section'=4,'dp'=8] {'dp'}, use_global_device_ids=true, to_apply=%region_2.2 | all-reduce | flops 128 | bytes 1024 | tf_op jit(solution)/shard_map/while/body/eval_jaxpr/psum | solution.py:40
  453.4 15.8 %reduce-scatter.5.cloned.1.call-done = f32[16,1024]{1,0:T(8,128)} async-done(((f32[128,1024]{1,0:T(8,128)}), f32[16,1024]{1,0:T(8,128)}) %reduce-scatter.5.cloned.1.call-update) | async-done | bytes 65552 | tf_op jit(solution)/shard_map/while/body/eval_jaxpr/reduce_scatter | solution.py:42
  470.1 14.2 %all_gather.11 = bf16[128,1024]{1,0:T(8,128)(2,1)S(1)} all-gather(bf16[16,1024]{1,0:T(8,128)(2,1)S(1)} %multiply_convert_fusion.2), channel_id=1, replica_groups=mesh['section'=4,'dp'=8] {'dp'}, dimensions={0}, use_global_device_ids=true | all-gather | bytes 294912 | tf_op jit(solution)/shard_map/while/body/eval_jaxpr/all_gather | solution.py:50
  491.5 8.2 select_add_fusion.2
  508.2 13.7 %psum.15 = f32[128]{0:T(128)S(1)} all-reduce(f32[128]{0:T(128)S(1)} %get-tuple-element.414), channel_id=1, replica_groups=mesh['section'=4,'dp'=8] {'dp'}, use_global_device_ids=true, to_apply=%region_2.2 | all-reduce | flops 128 | bytes 1024 | tf_op jit(solution)/shard_map/while/body/eval_jaxpr/psum | solution.py:40
  523.0 15.8 %reduce-scatter.5.cloned.1.call-done = f32[16,1024]{1,0:T(8,128)} async-done(((f32[128,1024]{1,0:T(8,128)}), f32[16,1024]{1,0:T(8,128)}) %reduce-scatter.5.cloned.1.call-update) | async-done | bytes 65552 | tf_op jit(solution)/shard_map/while/body/eval_jaxpr/reduce_scatter | solution.py:42
  539.8 14.2 %all_gather.11 = bf16[128,1024]{1,0:T(8,128)(2,1)S(1)} all-gather(bf16[16,1024]{1,0:T(8,128)(2,1)S(1)} %multiply_convert_fusion.2), channel_id=1, replica_groups=mesh['section'=4,'dp'=8] {'dp'}, dimensions={0}, use_global_device_ids=true | all-gather | bytes 294912 | tf_op jit(solution)/shard_map/while/body/eval_jaxpr/all_gather | solution.py:50
  561.2 8.2 select_add_fusion.2
  577.9 13.6 %psum.15 = f32[128]{0:T(128)S(1)} all-reduce(f32[128]{0:T(128)S(1)} %get-tuple-element.414), channel_id=1, replica_groups=mesh['section'=4,'dp'=8] {'dp'}, use_global_device_ids=true, to_apply=%region_2.2 | all-reduce | flops 128 | bytes 1024 | tf_op jit(solution)/shard_map/while/body/eval_jaxpr/psum | solution.py:40
  592.7 16.1 %reduce-scatter.5.cloned.1.call-done = f32[16,1024]{1,0:T(8,128)} async-done(((f32[128,1024]{1,0:T(8,128)}), f32[16,1024]{1,0:T(8,128)}) %reduce-scatter.5.cloned.1.call-update) | async-done | bytes 65552 | tf_op jit(solution)/shard_map/while/body/eval_jaxpr/reduce_scatter | solution.py:42
  609.7 14.2 %all_gather.11 = bf16[128,1024]{1,0:T(8,128)(2,1)S(1)} all-gather(bf16[16,1024]{1,0:T(8,128)(2,1)S(1)} %multiply_convert_fusion.2), channel_id=1, replica_groups=mesh['section'=4,'dp'=8] {'dp'}, dimensions={0}, use_global_device_ids=true | all-gather | bytes 294912 | tf_op jit(solution)/shard_map/while/body/eval_jaxpr/all_gather | solution.py:50
  631.0 8.2 select_add_fusion.2
  647.7 13.6 %psum.15 = f32[128]{0:T(128)S(1)} all-reduce(f32[128]{0:T(128)S(1)} %get-tuple-element.414), channel_id=1, replica_groups=mesh['section'=4,'dp'=8] {'dp'}, use_global_device_ids=true, to_apply=%region_2.2 | all-reduce | flops 128 | bytes 1024 | tf_op jit(solution)/shard_map/while/body/eval_jaxpr/psum | solution.py:40
  662.5 16.0 %reduce-scatter.5.cloned.1.call-done = f32[16,1024]{1,0:T(8,128)} async-done(((f32[128,1024]{1,0:T(8,128)}), f32[16,1024]{1,0:T(8,128)}) %reduce-scatter.5.cloned.1.call-update) | async-done | bytes 65552 | tf_op jit(solution)/shard_map/while/body/eval_jaxpr/reduce_scatter | solution.py:42
  679.4 14.2 %all_gather.11 = bf16[128,1024]{1,0:T(8,128)(2,1)S(1)} all-gather(bf16[16,1024]{1,0:T(8,128)(2,1)S(1)} %multiply_convert_fusion.2), channel_id=1, replica_groups=mesh['section'=4,'dp'=8] {'dp'}, dimensions={0}, use_global_device_ids=true | all-gather | bytes 294912 | tf_op jit(solution)/shard_map/while/body/eval_jaxpr/all_gather | solution.py:50
  700.8 8.2 select_add_fusion.2
  717.5 13.6 %psum.15 = f32[128]{0:T(128)S(1)} all-reduce(f32[128]{0:T(128)S(1)} %get-tuple-element.414), channel_id=1, replica_groups=mesh['section'=4,'dp'=8] {'dp'}, use_global_device_ids=true, to_apply=%region_2.2 | all-reduce | flops 128 | bytes 1024 | tf_op jit(solution)/shard_map/while/body/eval_jaxpr/psum | solution.py:40
  732.3 15.8 %reduce-scatter.5.cloned.1.call-done = f32[16,1024]{1,0:T(8,128)} async-done(((f32[128,1024]{1,0:T(8,128)}), f32[16,1024]{1,0:T(8,128)}) %reduce-scatter.5.cloned.1.call-update) | async-done | bytes 65552 | tf_op jit(solution)/shard_map/while/body/eval_jaxpr/reduce_scatter | solution.py:42
  749.1 14.2 %all_gather.11 = bf16[128,1024]{1,0:T(8,128)(2,1)S(1)} all-gather(bf16[16,1024]{1,0:T(8,128)(2,1)S(1)} %multiply_convert_fusion.2), channel_id=1, replica_groups=mesh['section'=4,'dp'=8] {'dp'}, dimensions={0}, use_global_device_ids=true | all-gather | bytes 294912 | tf_op jit(solution)/shard_map/while/body/eval_jaxpr/all_gather | solution.py:50
  770.6 8.2 select_add_fusion.2
  788.3 5.8 convolution_convert_fusion
  794.1 14.0 %fusion.12 = f32[1,2,1024,1024]{3,2,1,0:T(8,128)} fusion(f32[1,2,1024,1024]{3,2,1,0:T(8,128)} %param.14, bf16[2,1024,1024]{2,1,0:T(8,128)(2,1)} %bitcast.55), kind=kOutput, calls=%fused_computation.21 | convolution fusion | flops 4299161600 | bytes 20971520 | tf_op jit(solution)/shard_map/bik,bjk->bij/dot_general | solution.py:89
  808.1 21.4 %reduce-scatter.3.cloned.1.call-done = bf16[128,1024]{1,0:T(8,128)(2,1)} async-done(((bf16[1024,1024]{1,0:T(8,128)(2,1)}), bf16[128,1024]{1,0:T(8,128)(2,1)}) %reduce-scatter.3.cloned.1.call-update) | async-done | bytes 262160 | tf_op jit(solution)/shard_map/reduce_scatter | solution.py:91
  (133 shorter events, 209.2 us)
Async XLA Ops:
  11.3 39.2 %reduce-scatter.5.cloned.1.call-start = ((), (), s32[]{:S(2)}) async-start(), calls=%async_computation.3 | async-start | bytes 589824 | tf_op jit(solution)/shard_map/while/body/eval_jaxpr/reduce_scatter | solution.py:42
  69.5 15.1 %collective-permute-start = (bf16[128,2048]{1,0:T(8,128)(2,1)S(1)}, bf16[128,2048]{1,0:T(8,128)(2,1)S(1)}, u32[]{:S(2)}, u32[]{:S(2)}) collective-permute-start(bf16[128,2048]{1,0:T(8,128)(2,1)S(1)} %get-tuple-element.415), channel_id=1, source_target_pairs={{0,8},{8,16},{16,24},{1,9},{9,17},{17,25},{2,10},{10,18},{18,26},{... | collective-permute-start | bytes 1572872 | tf_op jit(solution)/shard_map/while/body/eval_jaxpr/ppermute | solution.py:13
  84.6 35.7 %reduce-scatter.5.cloned.1.call-start = ((), (), s32[]{:S(2)}) async-start(), calls=%async_computation.3 | async-start | bytes 589824 | tf_op jit(solution)/shard_map/while/body/eval_jaxpr/reduce_scatter | solution.py:42
  139.2 15.1 %collective-permute-start = (bf16[128,2048]{1,0:T(8,128)(2,1)S(1)}, bf16[128,2048]{1,0:T(8,128)(2,1)S(1)}, u32[]{:S(2)}, u32[]{:S(2)}) collective-permute-start(bf16[128,2048]{1,0:T(8,128)(2,1)S(1)} %get-tuple-element.415), channel_id=1, source_target_pairs={{0,8},{8,16},{16,24},{1,9},{9,17},{17,25},{2,10},{10,18},{18,26},{... | collective-permute-start | bytes 1572872 | tf_op jit(solution)/shard_map/while/body/eval_jaxpr/ppermute | solution.py:13
  154.3 35.8 %reduce-scatter.5.cloned.1.call-start = ((), (), s32[]{:S(2)}) async-start(), calls=%async_computation.3 | async-start | bytes 589824 | tf_op jit(solution)/shard_map/while/body/eval_jaxpr/reduce_scatter | solution.py:42
  209.0 15.0 %collective-permute-start = (bf16[128,2048]{1,0:T(8,128)(2,1)S(1)}, bf16[128,2048]{1,0:T(8,128)(2,1)S(1)}, u32[]{:S(2)}, u32[]{:S(2)}) collective-permute-start(bf16[128,2048]{1,0:T(8,128)(2,1)S(1)} %get-tuple-element.415), channel_id=1, source_target_pairs={{0,8},{8,16},{16,24},{1,9},{9,17},{17,25},{2,10},{10,18},{18,26},{... | collective-permute-start | bytes 1572872 | tf_op jit(solution)/shard_map/while/body/eval_jaxpr/ppermute | solution.py:13
  224.1 35.7 %reduce-scatter.5.cloned.1.call-start = ((), (), s32[]{:S(2)}) async-start(), calls=%async_computation.3 | async-start | bytes 589824 | tf_op jit(solution)/shard_map/while/body/eval_jaxpr/reduce_scatter | solution.py:42
  278.7 15.1 %collective-permute-start = (bf16[128,2048]{1,0:T(8,128)(2,1)S(1)}, bf16[128,2048]{1,0:T(8,128)(2,1)S(1)}, u32[]{:S(2)}, u32[]{:S(2)}) collective-permute-start(bf16[128,2048]{1,0:T(8,128)(2,1)S(1)} %get-tuple-element.415), channel_id=1, source_target_pairs={{0,8},{8,16},{16,24},{1,9},{9,17},{17,25},{2,10},{10,18},{18,26},{... | collective-permute-start | bytes 1572872 | tf_op jit(solution)/shard_map/while/body/eval_jaxpr/ppermute | solution.py:13
  293.8 35.7 %reduce-scatter.5.cloned.1.call-start = ((), (), s32[]{:S(2)}) async-start(), calls=%async_computation.3 | async-start | bytes 589824 | tf_op jit(solution)/shard_map/while/body/eval_jaxpr/reduce_scatter | solution.py:42
  348.4 15.1 %collective-permute-start = (bf16[128,2048]{1,0:T(8,128)(2,1)S(1)}, bf16[128,2048]{1,0:T(8,128)(2,1)S(1)}, u32[]{:S(2)}, u32[]{:S(2)}) collective-permute-start(bf16[128,2048]{1,0:T(8,128)(2,1)S(1)} %get-tuple-element.415), channel_id=1, source_target_pairs={{0,8},{8,16},{16,24},{1,9},{9,17},{17,25},{2,10},{10,18},{18,26},{... | collective-permute-start | bytes 1572872 | tf_op jit(solution)/shard_map/while/body/eval_jaxpr/ppermute | solution.py:13
  363.5 35.8 %reduce-scatter.5.cloned.1.call-start = ((), (), s32[]{:S(2)}) async-start(), calls=%async_computation.3 | async-start | bytes 589824 | tf_op jit(solution)/shard_map/while/body/eval_jaxpr/reduce_scatter | solution.py:42
  418.3 15.1 %collective-permute-start = (bf16[128,2048]{1,0:T(8,128)(2,1)S(1)}, bf16[128,2048]{1,0:T(8,128)(2,1)S(1)}, u32[]{:S(2)}, u32[]{:S(2)}) collective-permute-start(bf16[128,2048]{1,0:T(8,128)(2,1)S(1)} %get-tuple-element.415), channel_id=1, source_target_pairs={{0,8},{8,16},{16,24},{1,9},{9,17},{17,25},{2,10},{10,18},{18,26},{... | collective-permute-start | bytes 1572872 | tf_op jit(solution)/shard_map/while/body/eval_jaxpr/ppermute | solution.py:13
  433.5 35.7 %reduce-scatter.5.cloned.1.call-start = ((), (), s32[]{:S(2)}) async-start(), calls=%async_computation.3 | async-start | bytes 589824 | tf_op jit(solution)/shard_map/while/body/eval_jaxpr/reduce_scatter | solution.py:42
  488.1 15.0 %collective-permute-start = (bf16[128,2048]{1,0:T(8,128)(2,1)S(1)}, bf16[128,2048]{1,0:T(8,128)(2,1)S(1)}, u32[]{:S(2)}, u32[]{:S(2)}) collective-permute-start(bf16[128,2048]{1,0:T(8,128)(2,1)S(1)} %get-tuple-element.415), channel_id=1, source_target_pairs={{0,8},{8,16},{16,24},{1,9},{9,17},{17,25},{2,10},{10,18},{18,26},{... | collective-permute-start | bytes 1572872 | tf_op jit(solution)/shard_map/while/body/eval_jaxpr/ppermute | solution.py:13
  503.1 35.7 %reduce-scatter.5.cloned.1.call-start = ((), (), s32[]{:S(2)}) async-start(), calls=%async_computation.3 | async-start | bytes 589824 | tf_op jit(solution)/shard_map/while/body/eval_jaxpr/reduce_scatter | solution.py:42
  557.8 15.1 %collective-permute-start = (bf16[128,2048]{1,0:T(8,128)(2,1)S(1)}, bf16[128,2048]{1,0:T(8,128)(2,1)S(1)}, u32[]{:S(2)}, u32[]{:S(2)}) collective-permute-start(bf16[128,2048]{1,0:T(8,128)(2,1)S(1)} %get-tuple-element.415), channel_id=1, source_target_pairs={{0,8},{8,16},{16,24},{1,9},{9,17},{17,25},{2,10},{10,18},{18,26},{... | collective-permute-start | bytes 1572872 | tf_op jit(solution)/shard_map/while/body/eval_jaxpr/ppermute | solution.py:13
  572.8 35.9 %reduce-scatter.5.cloned.1.call-start = ((), (), s32[]{:S(2)}) async-start(), calls=%async_computation.3 | async-start | bytes 589824 | tf_op jit(solution)/shard_map/while/body/eval_jaxpr/reduce_scatter | solution.py:42
  627.7 14.9 %collective-permute-start = (bf16[128,2048]{1,0:T(8,128)(2,1)S(1)}, bf16[128,2048]{1,0:T(8,128)(2,1)S(1)}, u32[]{:S(2)}, u32[]{:S(2)}) collective-permute-start(bf16[128,2048]{1,0:T(8,128)(2,1)S(1)} %get-tuple-element.415), channel_id=1, source_target_pairs={{0,8},{8,16},{16,24},{1,9},{9,17},{17,25},{2,10},{10,18},{18,26},{... | collective-permute-start | bytes 1572872 | tf_op jit(solution)/shard_map/while/body/eval_jaxpr/ppermute | solution.py:13
  642.6 35.8 %reduce-scatter.5.cloned.1.call-start = ((), (), s32[]{:S(2)}) async-start(), calls=%async_computation.3 | async-start | bytes 589824 | tf_op jit(solution)/shard_map/while/body/eval_jaxpr/reduce_scatter | solution.py:42
  697.4 15.1 %collective-permute-start = (bf16[128,2048]{1,0:T(8,128)(2,1)S(1)}, bf16[128,2048]{1,0:T(8,128)(2,1)S(1)}, u32[]{:S(2)}, u32[]{:S(2)}) collective-permute-start(bf16[128,2048]{1,0:T(8,128)(2,1)S(1)} %get-tuple-element.415), channel_id=1, source_target_pairs={{0,8},{8,16},{16,24},{1,9},{9,17},{17,25},{2,10},{10,18},{18,26},{... | collective-permute-start | bytes 1572872 | tf_op jit(solution)/shard_map/while/body/eval_jaxpr/ppermute | solution.py:13
  712.5 35.7 %reduce-scatter.5.cloned.1.call-start = ((), (), s32[]{:S(2)}) async-start(), calls=%async_computation.3 | async-start | bytes 589824 | tf_op jit(solution)/shard_map/while/body/eval_jaxpr/reduce_scatter | solution.py:42
  767.1 15.2 %collective-permute-start = (bf16[128,2048]{1,0:T(8,128)(2,1)S(1)}, bf16[128,2048]{1,0:T(8,128)(2,1)S(1)}, u32[]{:S(2)}, u32[]{:S(2)}) collective-permute-start(bf16[128,2048]{1,0:T(8,128)(2,1)S(1)} %get-tuple-element.415), channel_id=1, source_target_pairs={{0,8},{8,16},{16,24},{1,9},{9,17},{17,25},{2,10},{10,18},{18,26},{... | collective-permute-start | bytes 1572872 | tf_op jit(solution)/shard_map/while/body/eval_jaxpr/ppermute | solution.py:13
  782.3 47.3 %reduce-scatter.3.cloned.1.call-start = ((), (), s32[]{:S(2)}) async-start(), calls=%async_computation.2 | async-start | bytes 2359296 | tf_op jit(solution)/shard_map/reduce_scatter | solution.py:91
  786.3 1.9 copy-start
  794.1 35.4 %copy-start.1 = (f32[1,128,1024]{2,1,0:T(8,128)S(1)}, f32[1,128,1024]{2,1,0:T(8,128)}, u32[]{:S(2)}) copy-start(f32[1,128,1024]{2,1,0:T(8,128)} %param.15) | copy-start | bytes 1572868
Sparse Core Ops, SparseCore 0:
  16.5 34.0 reduce-scatter.4
  89.7 30.5 reduce-scatter.4
  159.4 30.5 reduce-scatter.4
  229.2 30.5 reduce-scatter.4
  298.9 30.5 reduce-scatter.4
  368.7 30.6 reduce-scatter.4
  438.6 30.5 reduce-scatter.4
  508.3 30.5 reduce-scatter.4
  578.0 30.6 reduce-scatter.4
  647.8 30.6 reduce-scatter.4
  717.6 30.5 reduce-scatter.4
Sparse Core Ops, SparseCore 1:
  794.2 35.3 reduce-scatter.2
where the time goes:
time: 842 us; the launch traced here: 839 us
  blocking collectives  310 us (37%)
  waiting for transfers between devices  236 us (28%)
  matrix products  191 us (23%)
  starting transfers between devices  37.5 us (4%)
  other arithmetic  31.1 us (4%)
  local copies, waits for them, and re-layouts  17.3 us (2%)
  between operations  15.2 us (2%)
    reduce_scatter x11, waiting for transfers between devices, apply_layer(): lax.psum_scatter(jnp.dot(scaled_in, w_value, preferred_element_type=jnp.f...  174 us
    all_gather x11, blocking collectives, apply_layer(): values = lax.all_gather(value_own, 'dp', axis=0, tiled=True)  156 us
    psum x11, blocking collectives, apply_layer(): row_total = lax.psum(squares, 'dp')  154 us
    dot_general x11, matrix products, run_tick(): lax.dot_general(scaled_in, weighted, contract_rows, preferred_element_typ...  87.8 us
    dot_general x11, matrix products, apply_layer(): jnp.dot(values, w_output, preferred_element_type=jnp.float32)  42.4 us
    dot_general x11, matrix products, apply_layer(): jnp.dot(scaled_in, w_value, preferred_element_type=jnp.float32)  40.7 us
    ppermute x11, waiting for transfers between devices, passed_along(): lax.ppermute(value, axis, [(source, source + steps) for source in range(i...  40.3 us
    ppermute x11, starting transfers between devices, passed_along(): lax.ppermute(value, axis, [(source, source + steps) for source in range(i...  37.5 us
  transfers between devices with their start and end apart: 23, of which 23 were waited for; matrix products, arithmetic and copies ran while one was open for 14% of the time, Pallas kernels for 0%

commit v1 on v0

v1 whole, which is shorter than its diff:
```python
import functools

import jax
import jax.numpy as jnp
from jax import lax
from jax.experimental import pallas as pl
from jax.experimental.pallas import tpu as pltpu
from jax.sharding import PartitionSpec as P


BLOCK = 1024
LANES = 128
LAG = 3
TILE = 256


def swap(value, axis, mask):
    count = lax.axis_size(axis)
    return lax.ppermute(value, axis, [(i, i ^ mask) for i in range(count)])


def passed_along(value, axis):
    count = lax.axis_size(axis)
    return lax.ppermute(value, axis, [(i, i + 1) for i in range(count - 1)])


def put_pair(ref, total):
    high = total.astype(jnp.bfloat16)
    low = (total - high.astype(jnp.float32)).astype(jnp.bfloat16)
    rows = total.shape[0]
    lane = lax.broadcasted_iota(jnp.int32, (rows, LANES), 1)
    high = jnp.broadcast_to(high.astype(jnp.float32), (rows, LANES))
    low = jnp.broadcast_to(low.astype(jnp.float32), (rows, LANES))
    ref[...] = jnp.where(lane < LANES // 2, high, low).astype(jnp.bfloat16)


def get_pair(block):
    wide = block.astype(jnp.float32)
    return wide[:, :1] + wide[:, LANES // 2 : LANES // 2 + 1]


def project_kernel(first, where_ref, entering_ref, moved_ref, gain_ref, weight_ref, *rest):
    keep_ref, send_ref = rest[-2:]
    rows, wide = keep_ref.shape
    half = wide - LANES
    start = entering_ref[first * rows : (first + 1) * rows, :]
    hidden = jnp.where(where_ref[0] == 0, start, moved_ref[...]).astype(jnp.float32)
    scaled = (hidden * gain_ref[...].astype(jnp.float32)).astype(jnp.bfloat16)
    square = jnp.sum(hidden * hidden, axis=1, keepdims=True)
    put_pair(keep_ref.at[:, half:], square)
    put_pair(send_ref.at[:, half:], square)
    own = pl.multiple_of(where_ref[1] * half, LANES)
    theirs = pl.multiple_of((1 - where_ref[1]) * half, LANES)
    tile = min(TILE, half)
    for ref, first_col in ((send_ref, theirs), (keep_ref, own)):

        @pl.loop(0, half // tile)
        def _(index):
            at = pl.multiple_of(index * tile, LANES)
            ref[:, pl.ds(at, tile)] = jnp.dot(
                scaled, weight_ref[:, pl.ds(first_col + at, tile)], preferred_element_type=jnp.float32
            ).astype(jnp.bfloat16)


def join_kernel(mine_ref, other_ref, out_ref):
    half = out_ref.shape[1] - LANES
    out_ref[:, :half] = (
        mine_ref[:, :half].astype(jnp.float32) + other_ref[:, :half].astype(jnp.float32)
    ).astype(jnp.bfloat16)
    put_pair(out_ref.at[:, half:], get_pair(mine_ref[:, half:]) + get_pair(other_ref[:, half:]))


def value_kernel(pairs, model_width, *refs):
    parts, out_ref = refs[:pairs], refs[-1]
    half = out_ref.shape[1] - LANES
    total = parts[0][:, :half].astype(jnp.float32)
    square = get_pair(parts[0][:, half:])
    for part in parts[1:]:
        total += part[:, :half].astype(jnp.float32)
        square += get_pair(part[:, half:])
    inv_rms = lax.rsqrt(square / model_width + 0.25)
    out_ref[:, :half] = (inv_rms * total).astype(jnp.bfloat16)
    put_pair(out_ref.at[:, half:], inv_rms)


def output_kernel(first, slot, count, where_ref, mine_ref, other_ref, entering_ref, moved_ref, gain_ref, weight_ref, cotan_ref, *rest):
    result_ref, out_ref, scaled_ref, weighted_ref, values, cotan, scaled, weighted, sems = rest[-9:]
    rows, wide = mine_ref.shape
    half = wide - LANES
    at = pl.ds(pl.multiple_of(jnp.clip(slot - LAG * where_ref[0], 0, count - 1) * rows, 16), rows)
    fetch = pltpu.make_async_copy(cotan_ref.at[at, :], cotan, sems.at[0])
    fetch.start()
    values[:, pl.ds(pl.multiple_of(where_ref[1] * half, LANES), half)] = mine_ref[:, :half]
    values[:, pl.ds(pl.multiple_of((1 - where_ref[1]) * half, LANES), half)] = other_ref[:, :half]
    held_rows = pl.ds(first * rows, rows)
    tile = min(2 * TILE, result_ref.shape[1])

    @pl.loop(0, result_ref.shape[1] // tile)
    def _(index):
        part = pl.ds(pl.multiple_of(index * tile, LANES), tile)
        hidden = jnp.where(where_ref[0] == 0, entering_ref[held_rows, part], moved_ref[:, part]).astype(jnp.float32)
        scaled[:, part] = (hidden * gain_ref[:, part].astype(jnp.float32)).astype(jnp.bfloat16)
        result_ref[:, part] = (
            hidden + jnp.dot(values[...], weight_ref[:, part], preferred_element_type=jnp.float32)
        ).astype(jnp.bfloat16)

    store_scaled = pltpu.make_async_copy(scaled, scaled_ref.at[at, :], sems.at[1])
    store_scaled.start()
    store_out = pltpu.make_async_copy(result_ref, out_ref.at[at, :], sems.at[2])
    store_out.start()
    fetch.wait()
    weighted[...] = (get_pair(mine_ref[:, half:]) * cotan[...].astype(jnp.float32)).astype(jnp.bfloat16)
    store_weighted = pltpu.make_async_copy(weighted, weighted_ref.at[at, :], sems.at[3])
    store_weighted.start()
    store_scaled.wait()
    store_out.wait()
    store_weighted.wait()


def local_call(kernel, outs, operands, remote=(), aliases=None, scratch=(), limit=16):
    vmem = pl.BlockSpec(memory_space=pltpu.VMEM)
    hbm = pl.BlockSpec(memory_space=pl.ANY)
    scalars = 1 if operands[0].dtype == jnp.int32 else 0
    held = [pltpu.with_memory_space_constraint(x, pltpu.VMEM) for x in operands[scalars:]]
    near = [o for o in outs if not isinstance(o, tuple)]
    far = [pltpu.HBM(*o) for o in outs if isinstance(o, tuple)]
    return pl.pallas_call(
        kernel,
        out_shape=tuple([pltpu.VMEM(o.shape, o.dtype) for o in near] + far),
        in_specs=[pl.BlockSpec(memory_space=pltpu.SMEM)] * scalars + [vmem] * len(held) + [hbm] * len(remote),
        out_specs=(vmem,) * len(near) + (hbm,) * len(far),
        scratch_shapes=scratch,
        input_output_aliases=aliases or {},
        compiler_params=pltpu.CompilerParams(vmem_limit_bytes=limit << 20),
    )(*operands[:scalars], *held, *remote)


def on_device(inputs, cotangent, norm_gain, value_weight, output_weight, left_old, right_old):
    sections = lax.axis_size("section")
    dp_count = lax.axis_size("dp")
    section_index = lax.axis_index("section")
    owner_index = lax.axis_index("dp")
    core_index = owner_index % 2
    pair_index = owner_index // 2
    pairs = dp_count // 2
    micro_count, rows, cols = inputs.shape
    width_kv = value_weight.shape[2]
    half = width_kv // 2
    wide = half + LANES
    tokens = micro_count * rows
    entering = inputs.reshape(tokens, cols)
    cotan = cotangent.reshape(tokens, width_kv)
    w_value = value_weight[0]
    w_output = output_weight[0]
    where_am_i = jnp.stack([section_index, core_index]).astype(jnp.int32)
    count = micro_count
    slots = count + LAG * (sections - 1)
    bf16 = lambda *shape: jax.ShapeDtypeStruct(shape, jnp.bfloat16)
    message = bf16(rows, wide)

    def project(slot, moved, behind):
        first = min(slot, count - 1)
        return local_call(
            functools.partial(project_kernel, first),
            (message, message),
            (where_am_i, entering, moved, norm_gain, w_value) + (() if behind is None else (behind,)),
        )

    def emit(slot, mine, other, moved, buffers):
        first = min(slot, count - 1)
        operands = (where_am_i, mine, other, entering, moved, norm_gain, w_output)
        aliases = {len(operands) + 1 + i: 1 + i for i in range(len(buffers))}
        big = ((tokens, cols), jnp.bfloat16)
        narrow = ((tokens, width_kv), jnp.bfloat16)
        return local_call(
            functools.partial(output_kernel, first, slot, count),
            (bf16(rows, cols), big, big, narrow),
            operands,
            (cotan,) + buffers,
            aliases,
            (
                pltpu.VMEM((rows, width_kv), jnp.bfloat16),
                pltpu.VMEM((rows, width_kv), jnp.bfloat16),
                pltpu.VMEM((rows, cols), jnp.bfloat16),
                pltpu.VMEM((rows, width_kv), jnp.bfloat16),
                pltpu.SemaphoreType.DMA((4,)),
            ),
        )

    buffers = ()
    moved = [jnp.zeros((rows, cols), jnp.bfloat16)] * LAG
    waiting = None
    behind = None
    for slot in range(slots + 1):
        if slot < slots:
            keep, send = project(slot, moved[slot], behind)
            (pair_sum,) = local_call(join_kernel, (message,), (keep, swap(send, "dp", 1)))
            entered = [pair_sum] + [swap(pair_sum, "dp", 2 * mask) for mask in range(1, pairs)]
        if slot > 0:
            (mine,) = local_call(
                functools.partial(value_kernel, pairs, cols * dp_count), (message,), waiting + [pair_sum]
            )
            behind, *buffers = emit(slot - 1, mine, swap(mine, "dp", 1), moved[slot - 1], tuple(buffers))
            if slot - 1 + LAG < slots:
                moved.append(passed_along(behind, "section"))
        waiting = entered

    outputs_buf, scaled_all, weighted_all = buffers
    contract_rows = (((0,), (0,)), ((), ()))
    gradient = lax.dot_general(
        scaled_all, weighted_all, contract_rows, preferred_element_type=jnp.float32
    ).astype(jnp.bfloat16)

    share = width_kv // dp_count
    right_part = (
        lax.dot_general(gradient, gradient, contract_rows, preferred_element_type=jnp.float32)
        .astype(jnp.bfloat16)
        .reshape(pairs, 2, share, width_kv)
    )
    theirs = lax.dynamic_index_in_dim(right_part, 1 - core_index, 1, keepdims=False)
    ours = lax.dynamic_index_in_dim(right_part, core_index, 1, keepdims=False)
    from_core = swap(theirs, "dp", 1)
    pair_right = ours.astype(jnp.float32) + from_core.astype(jnp.float32)

    def piece(mask):
        return lax.dynamic_index_in_dim(pair_right, pair_index ^ mask, 0, keepdims=False)

    right_rows = piece(0)
    for mask in range(1, pairs):
        right_rows = right_rows + swap(piece(mask).astype(jnp.bfloat16), "dp", 2 * mask).astype(jnp.float32)
    right_new = right_old[0] + right_rows / (cols * dp_count)

    blocks = gradient.reshape(cols // BLOCK, BLOCK, width_kv)
    left_new = (
        left_old[0]
        + jnp.einsum("bik,bjk->bij", blocks, blocks, preferred_element_type=jnp.float32) / BLOCK
    )
    return (outputs_buf.reshape(1, micro_count, rows, cols), left_new[None], right_new[None])


def solution(mesh):
    placed = (
        P(None, None, "dp"),
        P("section", None, None, None),
        P("section", "dp"),
        P("section", "dp", None),
        P("section", None, "dp"),
        P("section", "dp", None, None),
        P("section", "dp", None),
    )
    return jax.shard_map(
        on_device,
        mesh=mesh,
        in_specs=placed,
        out_specs=(
            P("section", None, None, "dp"),
            P("section", "dp", None, None),
            P("section", "dp", None),
        ),
        check_vma=False,
    )
```

time: 842 us -> 530 us (0.63)
  the two profiles are of different devices: /device:TPU:0 before, /device:TPU:16 now
where the time goes in v1:
time: 530 us; the launch traced here: 521 us
  waiting for transfers between devices  281 us (53%)
  starting transfers between devices  110 us (21%)
  Pallas kernels  94.4 us (18%)
  matrix products  21.3 us (4%)
  local copies, waits for them, and re-layouts  10.7 us (2%)
    ppermute x89, waiting for transfers between devices, swap(): return lax.ppermute(value, axis, [(i, i ^ mask) for i in range(count)])  281 us
    pallas_call x68, Pallas kernels, local_call(): pl.pallas_call(kernel, out_shape=tuple([pltpu.VMEM(o.shape, o.dtype) for...  94.4 us
    ppermute x89, starting transfers between devices, swap(): return lax.ppermute(value, axis, [(i, i ^ mask) for i in range(count)])  66.5 us
    ppermute x14, starting transfers between devices, passed_along(): return lax.ppermute(value, axis, [(i, i + 1) for i in range(count - 1)])  43.2 us
  transfers between devices with their start and end apart: 103, of which 68 were waited for; matrix products, arithmetic and copies ran while one was open for 2% of the time, Pallas kernels for 16%

profile of v1, /device:TPU:16, one launch (start us, length us, event | category | flops | bytes accessed | tf_op | source)
XLA Modules:
  0.0 521.4 jit_solution(2351071480179866107)
XLA Ops:
  14.8 3.8 collective-permute-done.5.refs_1_
  18.6 6.0 %collective-permute-done.6.refs_2_ = bf16[128,640]{1,0:T(8,128)(2,1)S(1)} collective-permute-done((bf16[128,640]{1,0:T(8,128)(2,1)S(1)}, bf16[128,640]{1,0:T(8,128)(2,1)S(1)}, u32[]{:S(2)}, u32[]{:S(2)}) %collective-permute-start.6) | collective-permute-done | bytes 163872 | tf_op jit(solution)/shard_map/ppermute | solution.py:19
  24.6 4.4 collective-permute-done.7.refs_3_
  33.6 3.4 collective-permute-start.15
  43.0 3.4 collective-permute-done.1.refs_1_
  46.4 6.5 %collective-permute-done.2.refs_2_ = bf16[128,640]{1,0:T(8,128)(2,1)S(1)} collective-permute-done((bf16[128,640]{1,0:T(8,128)(2,1)S(1)}, bf16[128,640]{1,0:T(8,128)(2,1)S(1)}, u32[]{:S(2)}, u32[]{:S(2)}) %collective-permute-start.2) | collective-permute-done | bytes 163872 | tf_op jit(solution)/shard_map/ppermute | solution.py:19
  52.9 4.7 collective-permute-done.3.refs_3_
  62.1 3.4 collective-permute-start.11
  74.9 6.5 %collective-permute-done.13.refs_2_ = bf16[128,640]{1,0:T(8,128)(2,1)S(1)} collective-permute-done((bf16[128,640]{1,0:T(8,128)(2,1)S(1)}, bf16[128,640]{1,0:T(8,128)(2,1)S(1)}, u32[]{:S(2)}, u32[]{:S(2)}) %collective-permute-start.13) | collective-permute-done | bytes 163872 | tf_op jit(solution)/shard_map/ppermute | solution.py:19
  81.4 4.7 collective-permute-done.14.refs_3_
  90.7 3.4 collective-permute-start.22
  103.5 6.5 %collective-permute-done.24.refs_2_ = bf16[128,640]{1,0:T(8,128)(2,1)S(1)} collective-permute-done((bf16[128,640]{1,0:T(8,128)(2,1)S(1)}, bf16[128,640]{1,0:T(8,128)(2,1)S(1)}, u32[]{:S(2)}, u32[]{:S(2)}) %collective-permute-start.24) | collective-permute-done | bytes 163872 | tf_op jit(solution)/shard_map/ppermute | solution.py:19
  110.0 4.7 collective-permute-done.25.refs_3_
  130.6 6.5 %collective-permute-done.20.refs_2_ = bf16[128,640]{1,0:T(8,128)(2,1)S(1)} collective-permute-done((bf16[128,640]{1,0:T(8,128)(2,1)S(1)}, bf16[128,640]{1,0:T(8,128)(2,1)S(1)}, u32[]{:S(2)}, u32[]{:S(2)}) %collective-permute-start.20) | collective-permute-done | bytes 163872 | tf_op jit(solution)/shard_map/ppermute | solution.py:19
  137.1 4.7 collective-permute-done.21.refs_3_
  146.4 13.5 %collective-permute-start.29 = (bf16[128,2048]{1,0:T(8,128)(2,1)S(1)}, bf16[128,2048]{1,0:T(8,128)(2,1)S(1)}, u32[]{:S(2)}, u32[]{:S(2)}) collective-permute-start(bf16[128,2048]{1,0:T(8,128)(2,1)S(1)} %get-tuple-element.131.rest_0_), channel_id=1, source_target_pairs={{0,8},{8,16},{16,24},{1,9},{9,17},{17,25},{2,10},{10,18},{18,26},{... | collective-permute-start | bytes 1572872 | tf_op jit(solution)/shard_map/ppermute | solution.py:24
  165.9 3.4 collective-permute-done.30.refs_1_
  169.2 6.5 %collective-permute-done.31.refs_2_ = bf16[128,640]{1,0:T(8,128)(2,1)S(1)} collective-permute-done((bf16[128,640]{1,0:T(8,128)(2,1)S(1)}, bf16[128,640]{1,0:T(8,128)(2,1)S(1)}, u32[]{:S(2)}, u32[]{:S(2)}) %collective-permute-start.31) | collective-permute-done | bytes 163872 | tf_op jit(solution)/shard_map/ppermute | solution.py:19
  175.7 4.8 collective-permute-done.32.refs_3_
  196.3 6.5 %collective-permute-done.42.refs_2_ = bf16[128,640]{1,0:T(8,128)(2,1)S(1)} collective-permute-done((bf16[128,640]{1,0:T(8,128)(2,1)S(1)}, bf16[128,640]{1,0:T(8,128)(2,1)S(1)}, u32[]{:S(2)}, u32[]{:S(2)}) %collective-permute-start.42) | collective-permute-done | bytes 163872 | tf_op jit(solution)/shard_map/ppermute | solution.py:19
  202.8 4.7 collective-permute-done.43.refs_3_
  223.4 6.5 %collective-permute-done.38.refs_2_ = bf16[128,640]{1,0:T(8,128)(2,1)S(1)} collective-permute-done((bf16[128,640]{1,0:T(8,128)(2,1)S(1)}, bf16[128,640]{1,0:T(8,128)(2,1)S(1)}, u32[]{:S(2)}, u32[]{:S(2)}) %collective-permute-start.38) | collective-permute-done | bytes 163872 | tf_op jit(solution)/shard_map/ppermute | solution.py:19
  229.9 4.7 collective-permute-done.39.refs_3_
  250.5 6.5 %collective-permute-done.49.refs_2_ = bf16[128,640]{1,0:T(8,128)(2,1)S(1)} collective-permute-done((bf16[128,640]{1,0:T(8,128)(2,1)S(1)}, bf16[128,640]{1,0:T(8,128)(2,1)S(1)}, u32[]{:S(2)}, u32[]{:S(2)}) %collective-permute-start.49) | collective-permute-done | bytes 163872 | tf_op jit(solution)/shard_map/ppermute | solution.py:19
  257.0 4.7 collective-permute-done.50.refs_3_
  277.6 6.5 %collective-permute-done.60.refs_2_ = bf16[128,640]{1,0:T(8,128)(2,1)S(1)} collective-permute-done((bf16[128,640]{1,0:T(8,128)(2,1)S(1)}, bf16[128,640]{1,0:T(8,128)(2,1)S(1)}, u32[]{:S(2)}, u32[]{:S(2)}) %collective-permute-start.60) | collective-permute-done | bytes 163872 | tf_op jit(solution)/shard_map/ppermute | solution.py:19
  284.1 4.7 collective-permute-done.61.refs_3_
  304.7 6.5 %collective-permute-done.56.refs_2_ = bf16[128,640]{1,0:T(8,128)(2,1)S(1)} collective-permute-done((bf16[128,640]{1,0:T(8,128)(2,1)S(1)}, bf16[128,640]{1,0:T(8,128)(2,1)S(1)}, u32[]{:S(2)}, u32[]{:S(2)}) %collective-permute-start.56) | collective-permute-done | bytes 163872 | tf_op jit(solution)/shard_map/ppermute | solution.py:19
  311.1 4.8 collective-permute-done.57.refs_3_
  328.4 3.4 collective-permute-done.66.refs_1_
  331.8 6.5 %collective-permute-done.67.refs_2_ = bf16[128,640]{1,0:T(8,128)(2,1)S(1)} collective-permute-done((bf16[128,640]{1,0:T(8,128)(2,1)S(1)}, bf16[128,640]{1,0:T(8,128)(2,1)S(1)}, u32[]{:S(2)}, u32[]{:S(2)}) %collective-permute-start.67) | collective-permute-done | bytes 163872 | tf_op jit(solution)/shard_map/ppermute | solution.py:19
  338.2 4.8 collective-permute-done.68.refs_3_
  358.9 6.5 %collective-permute-done.78.refs_2_ = bf16[128,640]{1,0:T(8,128)(2,1)S(1)} collective-permute-done((bf16[128,640]{1,0:T(8,128)(2,1)S(1)}, bf16[128,640]{1,0:T(8,128)(2,1)S(1)}, u32[]{:S(2)}, u32[]{:S(2)}) %collective-permute-start.78) | collective-permute-done | bytes 163872 | tf_op jit(solution)/shard_map/ppermute | solution.py:19
  365.3 4.8 collective-permute-done.79.refs_3_
  385.9 6.5 %collective-permute-done.74.refs_2_ = bf16[128,640]{1,0:T(8,128)(2,1)S(1)} collective-permute-done((bf16[128,640]{1,0:T(8,128)(2,1)S(1)}, bf16[128,640]{1,0:T(8,128)(2,1)S(1)}, u32[]{:S(2)}, u32[]{:S(2)}) %collective-permute-start.74) | collective-permute-done | bytes 163872 | tf_op jit(solution)/shard_map/ppermute | solution.py:19
  392.4 4.7 collective-permute-done.75.refs_3_
  413.2 6.5 %collective-permute-done.85.refs_2_ = bf16[128,640]{1,0:T(8,128)(2,1)S(1)} collective-permute-done((bf16[128,640]{1,0:T(8,128)(2,1)S(1)}, bf16[128,640]{1,0:T(8,128)(2,1)S(1)}, u32[]{:S(2)}, u32[]{:S(2)}) %collective-permute-start.85) | collective-permute-done | bytes 163872 | tf_op jit(solution)/shard_map/ppermute | solution.py:19
  419.7 4.8 collective-permute-done.86.refs_3_
  439.2 5.5 %collective-permute-done.96.refs_2_ = bf16[128,640]{1,0:T(8,128)(2,1)S(1)} collective-permute-done((bf16[128,640]{1,0:T(8,128)(2,1)S(1)}, bf16[128,640]{1,0:T(8,128)(2,1)S(1)}, u32[]{:S(2)}, u32[]{:S(2)}) %collective-permute-start.96) | collective-permute-done | bytes 163872 | tf_op jit(solution)/shard_map/ppermute | solution.py:19
  444.8 12.7 %collective-permute-done.97.refs_3_ = bf16[128,640]{1,0:T(8,128)(2,1)S(1)} collective-permute-done((bf16[128,640]{1,0:T(8,128)(2,1)S(1)}, bf16[128,640]{1,0:T(8,128)(2,1)S(1)}, u32[]{:S(2)}, u32[]{:S(2)}) %collective-permute-start.97) | collective-permute-done | bytes 163872 | tf_op jit(solution)/shard_map/ppermute | solution.py:19
  459.0 4.7 collective-permute-done.93.refs_3_
  468.3 4.1 shard_map.160
  472.4 4.1 shard_map.161
  476.5 7.4 %convolution_convert_fusion = bf16[2048,1024]{1,0:T(8,128)(2,1)S(1)} fusion(bf16[1024,2048]{1,0:T(8,128)(2,1)} %get-tuple-element.201, bf16[1024,1024]{1,0:T(8,128)(2,1)} %get-tuple-element.202), kind=kOutput, calls=%fused_computation.2 | convolution fusion | flops 4297064448 | bytes 10485760 | tf_op jit(solution)/shard_map/dot_general | solution.py:210
  483.9 4.8 convolution_convert_fusion.1
  496.9 9.1 %fusion = f32[1,2,1024,1024]{3,2,1,0:T(8,128)} fusion(f32[1,2,1024,1024]{3,2,1,0:T(8,128)} %param.12, bf16[2,1024,1024]{2,1,0:T(8,128)(2,1)S(1)} %bitcast.138), kind=kOutput, calls=%fused_computation.1 | convolution fusion | flops 4299161600 | bytes 20971520 | tf_op jit(solution)/shard_map/bik,bjk->bij/dot_general | solution.py:236
  506.0 7.3 %collective-permute-done.101 = bf16[128,1024]{1,0:T(8,128)(2,1)S(1)} collective-permute-done((bf16[128,1024]{1,0:T(8,128)(2,1)S(1)}, bf16[128,1024]{1,0:T(8,128)(2,1)S(1)}, u32[]{:S(2)}, u32[]{:S(2)}) %collective-permute-start.101) | collective-permute-done | bytes 262176 | tf_op jit(solution)/shard_map/ppermute | solution.py:19
  513.2 6.8 %collective-permute-done.102 = bf16[128,1024]{1,0:T(8,128)(2,1)S(1)} collective-permute-done((bf16[128,1024]{1,0:T(8,128)(2,1)S(1)}, bf16[128,1024]{1,0:T(8,128)(2,1)S(1)}, u32[]{:S(2)}, u32[]{:S(2)}) %collective-permute-start.102) | collective-permute-done | bytes 262176 | tf_op jit(solution)/shard_map/ppermute | solution.py:19
  (261 shorter events, 247.4 us)
Async XLA Ops:
  13.0 16.0 %collective-permute-start.7 = (bf16[128,640]{1,0:T(8,128)(2,1)S(1)}, bf16[128,640]{1,0:T(8,128)(2,1)S(1)}, u32[]{:S(2)}, u32[]{:S(2)}) collective-permute-start(bf16[128,640]{1,0:T(8,128)(2,1)S(1)} %shard_map.97.refs_0_), channel_id=1, source_target_pairs={{0,6},{1,7},{2,4},{3,5},{4,2},{5,3},{6,0},{7,1},{8,14},{9,15},{10,... | collective-permute-start | bytes 491528 | tf_op jit(solution)/shard_map/ppermute | solution.py:19
  33.6 32.0 %collective-permute-start.15 = (bf16[128,2048]{1,0:T(8,128)(2,1)S(1)}, bf16[128,2048]{1,0:T(8,128)(2,1)S(1)}, u32[]{:S(2)}, u32[]{:S(2)}) collective-permute-start(bf16[128,2048]{1,0:T(8,128)(2,1)S(1)} %get-tuple-element.107.rest_0_), channel_id=1, source_target_pairs={{0,8},{8,16},{16,24},{1,9},{9,17},{17,25},{2,10},{10,18},{18,26},{... | collective-permute-start | bytes 1572872 | tf_op jit(solution)/shard_map/ppermute | solution.py:24
  39.3 13.6 %collective-permute-start.2 = (bf16[128,640]{1,0:T(8,128)(2,1)S(1)}, bf16[128,640]{1,0:T(8,128)(2,1)S(1)}, u32[]{:S(2)}, u32[]{:S(2)}) collective-permute-start(bf16[128,640]{1,0:T(8,128)(2,1)S(1)} %shard_map.95.refs_4_.refs_0_), channel_id=1, source_target_pairs={{0,4},{1,5},{2,6},{3,7},{4,0},{5,1},{6,2},{7,3},{8,12},{9,13},{10,... | collective-permute-start | bytes 491528 | tf_op jit(solution)/shard_map/ppermute | solution.py:19
  41.2 16.4 %collective-permute-start.3 = (bf16[128,640]{1,0:T(8,128)(2,1)S(1)}, bf16[128,640]{1,0:T(8,128)(2,1)S(1)}, u32[]{:S(2)}, u32[]{:S(2)}) collective-permute-start(bf16[128,640]{1,0:T(8,128)(2,1)S(1)} %shard_map.95.refs_4_.refs_0_), channel_id=1, source_target_pairs={{0,6},{1,7},{2,4},{3,5},{4,2},{5,3},{6,0},{7,1},{8,14},{9,15},{10,... | collective-permute-start | bytes 491528 | tf_op jit(solution)/shard_map/ppermute | solution.py:19
  62.1 32.0 %collective-permute-start.11 = (bf16[128,2048]{1,0:T(8,128)(2,1)S(1)}, bf16[128,2048]{1,0:T(8,128)(2,1)S(1)}, u32[]{:S(2)}, u32[]{:S(2)}) collective-permute-start(bf16[128,2048]{1,0:T(8,128)(2,1)S(1)} %get-tuple-element.113.rest_0_), channel_id=1, source_target_pairs={{0,8},{8,16},{16,24},{1,9},{9,17},{17,25},{2,10},{10,18},{18,26},{... | collective-permute-start | bytes 1572872 | tf_op jit(solution)/shard_map/ppermute | solution.py:24
  67.9 13.6 %collective-permute-start.13 = (bf16[128,640]{1,0:T(8,128)(2,1)S(1)}, bf16[128,640]{1,0:T(8,128)(2,1)S(1)}, u32[]{:S(2)}, u32[]{:S(2)}) collective-permute-start(bf16[128,640]{1,0:T(8,128)(2,1)S(1)} %shard_map.101.refs_4_.refs_0_), channel_id=1, source_target_pairs={{0,4},{1,5},{2,6},{3,7},{4,0},{5,1},{6,2},{7,3},{8,12},{9,13},{10,... | collective-permute-start | bytes 491528 | tf_op jit(solution)/shard_map/ppermute | solution.py:19
  69.8 16.4 %collective-permute-start.14 = (bf16[128,640]{1,0:T(8,128)(2,1)S(1)}, bf16[128,640]{1,0:T(8,128)(2,1)S(1)}, u32[]{:S(2)}, u32[]{:S(2)}) collective-permute-start(bf16[128,640]{1,0:T(8,128)(2,1)S(1)} %shard_map.101.refs_4_.refs_0_), channel_id=1, source_target_pairs={{0,6},{1,7},{2,4},{3,5},{4,2},{5,3},{6,0},{7,1},{8,14},{9,15},{10,... | collective-permute-start | bytes 491528 | tf_op jit(solution)/shard_map/ppermute | solution.py:19
  90.7 30.5 %collective-permute-start.22 = (bf16[128,2048]{1,0:T(8,128)(2,1)S(1)}, bf16[128,2048]{1,0:T(8,128)(2,1)S(1)}, u32[]{:S(2)}, u32[]{:S(2)}) collective-permute-start(bf16[128,2048]{1,0:T(8,128)(2,1)S(1)} %get-tuple-element.119.rest_0_), channel_id=1, source_target_pairs={{0,8},{8,16},{16,24},{1,9},{9,17},{17,25},{2,10},{10,18},{18,26},{... | collective-permute-start | bytes 1572872 | tf_op jit(solution)/shard_map/ppermute | solution.py:24
  96.4 13.6 %collective-permute-start.24 = (bf16[128,640]{1,0:T(8,128)(2,1)S(1)}, bf16[128,640]{1,0:T(8,128)(2,1)S(1)}, u32[]{:S(2)}, u32[]{:S(2)}) collective-permute-start(bf16[128,640]{1,0:T(8,128)(2,1)S(1)} %shard_map.105.refs_4_.refs_0_), channel_id=1, source_target_pairs={{0,4},{1,5},{2,6},{3,7},{4,0},{5,1},{6,2},{7,3},{8,12},{9,13},{10,... | collective-permute-start | bytes 491528 | tf_op jit(solution)/shard_map/ppermute | solution.py:19
  98.3 16.4 %collective-permute-start.25 = (bf16[128,640]{1,0:T(8,128)(2,1)S(1)}, bf16[128,640]{1,0:T(8,128)(2,1)S(1)}, u32[]{:S(2)}, u32[]{:S(2)}) collective-permute-start(bf16[128,640]{1,0:T(8,128)(2,1)S(1)} %shard_map.105.refs_4_.refs_0_), channel_id=1, source_target_pairs={{0,6},{1,7},{2,4},{3,5},{4,2},{5,3},{6,0},{7,1},{8,14},{9,15},{10,... | collective-permute-start | bytes 491528 | tf_op jit(solution)/shard_map/ppermute | solution.py:19
  119.3 40.6 %collective-permute-start.33 = (bf16[128,2048]{1,0:T(8,128)(2,1)S(1)}, bf16[128,2048]{1,0:T(8,128)(2,1)S(1)}, u32[]{:S(2)}, u32[]{:S(2)}) collective-permute-start(bf16[128,2048]{1,0:T(8,128)(2,1)S(1)} %get-tuple-element.125.rest_0_), channel_id=1, source_target_pairs={{0,8},{8,16},{16,24},{1,9},{9,17},{17,25},{2,10},{10,18},{18,26},{... | collective-permute-start | bytes 1572872 | tf_op jit(solution)/shard_map/ppermute | solution.py:24
  123.5 13.5 %collective-permute-start.20 = (bf16[128,640]{1,0:T(8,128)(2,1)S(1)}, bf16[128,640]{1,0:T(8,128)(2,1)S(1)}, u32[]{:S(2)}, u32[]{:S(2)}) collective-permute-start(bf16[128,640]{1,0:T(8,128)(2,1)S(1)} %shard_map.109.refs_4_.refs_0_), channel_id=1, source_target_pairs={{0,4},{1,5},{2,6},{3,7},{4,0},{5,1},{6,2},{7,3},{8,12},{9,13},{10,... | collective-permute-start | bytes 491528 | tf_op jit(solution)/shard_map/ppermute | solution.py:19
  125.4 16.4 %collective-permute-start.21 = (bf16[128,640]{1,0:T(8,128)(2,1)S(1)}, bf16[128,640]{1,0:T(8,128)(2,1)S(1)}, u32[]{:S(2)}, u32[]{:S(2)}) collective-permute-start(bf16[128,640]{1,0:T(8,128)(2,1)S(1)} %shard_map.109.refs_4_.refs_0_), channel_id=1, source_target_pairs={{0,6},{1,7},{2,4},{3,5},{4,2},{5,3},{6,0},{7,1},{8,14},{9,15},{10,... | collective-permute-start | bytes 491528 | tf_op jit(solution)/shard_map/ppermute | solution.py:19
  146.4 40.6 %collective-permute-start.29 = (bf16[128,2048]{1,0:T(8,128)(2,1)S(1)}, bf16[128,2048]{1,0:T(8,128)(2,1)S(1)}, u32[]{:S(2)}, u32[]{:S(2)}) collective-permute-start(bf16[128,2048]{1,0:T(8,128)(2,1)S(1)} %get-tuple-element.131.rest_0_), channel_id=1, source_target_pairs={{0,8},{8,16},{16,24},{1,9},{9,17},{17,25},{2,10},{10,18},{18,26},{... | collective-permute-start | bytes 1572872 | tf_op jit(solution)/shard_map/ppermute | solution.py:24
  162.2 13.5 %collective-permute-start.31 = (bf16[128,640]{1,0:T(8,128)(2,1)S(1)}, bf16[128,640]{1,0:T(8,128)(2,1)S(1)}, u32[]{:S(2)}, u32[]{:S(2)}) collective-permute-start(bf16[128,640]{1,0:T(8,128)(2,1)S(1)} %shard_map.113.refs_4_.refs_0_), channel_id=1, source_target_pairs={{0,4},{1,5},{2,6},{3,7},{4,0},{5,1},{6,2},{7,3},{8,12},{9,13},{10,... | collective-permute-start | bytes 491528 | tf_op jit(solution)/shard_map/ppermute | solution.py:19
  164.1 16.4 %collective-permute-start.32 = (bf16[128,640]{1,0:T(8,128)(2,1)S(1)}, bf16[128,640]{1,0:T(8,128)(2,1)S(1)}, u32[]{:S(2)}, u32[]{:S(2)}) collective-permute-start(bf16[128,640]{1,0:T(8,128)(2,1)S(1)} %shard_map.113.refs_4_.refs_0_), channel_id=1, source_target_pairs={{0,6},{1,7},{2,4},{3,5},{4,2},{5,3},{6,0},{7,1},{8,14},{9,15},{10,... | collective-permute-start | bytes 491528 | tf_op jit(solution)/shard_map/ppermute | solution.py:19
  185.0 29.1 %collective-permute-start.40 = (bf16[128,2048]{1,0:T(8,128)(2,1)S(1)}, bf16[128,2048]{1,0:T(8,128)(2,1)S(1)}, u32[]{:S(2)}, u32[]{:S(2)}) collective-permute-start(bf16[128,2048]{1,0:T(8,128)(2,1)S(1)} %get-tuple-element.137.rest_0_), channel_id=1, source_target_pairs={{0,8},{8,16},{16,24},{1,9},{9,17},{17,25},{2,10},{10,18},{18,26},{... | collective-permute-start | bytes 1572872 | tf_op jit(solution)/shard_map/ppermute | solution.py:24
  189.3 13.5 %collective-permute-start.42 = (bf16[128,640]{1,0:T(8,128)(2,1)S(1)}, bf16[128,640]{1,0:T(8,128)(2,1)S(1)}, u32[]{:S(2)}, u32[]{:S(2)}) collective-permute-start(bf16[128,640]{1,0:T(8,128)(2,1)S(1)} %shard_map.117.refs_4_.refs_0_), channel_id=1, source_target_pairs={{0,4},{1,5},{2,6},{3,7},{4,0},{5,1},{6,2},{7,3},{8,12},{9,13},{10,... | collective-permute-start | bytes 491528 | tf_op jit(solution)/shard_map/ppermute | solution.py:19
  191.2 16.4 %collective-permute-start.43 = (bf16[128,640]{1,0:T(8,128)(2,1)S(1)}, bf16[128,640]{1,0:T(8,128)(2,1)S(1)}, u32[]{:S(2)}, u32[]{:S(2)}) collective-permute-start(bf16[128,640]{1,0:T(8,128)(2,1)S(1)} %shard_map.117.refs_4_.refs_0_), channel_id=1, source_target_pairs={{0,6},{1,7},{2,4},{3,5},{4,2},{5,3},{6,0},{7,1},{8,14},{9,15},{10,... | collective-permute-start | bytes 491528 | tf_op jit(solution)/shard_map/ppermute | solution.py:19
  212.1 29.0 %collective-permute-start.51 = (bf16[128,2048]{1,0:T(8,128)(2,1)S(1)}, bf16[128,2048]{1,0:T(8,128)(2,1)S(1)}, u32[]{:S(2)}, u32[]{:S(2)}) collective-permute-start(bf16[128,2048]{1,0:T(8,128)(2,1)S(1)} %get-tuple-element.143.rest_0_), channel_id=1, source_target_pairs={{0,8},{8,16},{16,24},{1,9},{9,17},{17,25},{2,10},{10,18},{18,26},{... | collective-permute-start | bytes 1572872 | tf_op jit(solution)/shard_map/ppermute | solution.py:24
  216.4 13.5 %collective-permute-start.38 = (bf16[128,640]{1,0:T(8,128)(2,1)S(1)}, bf16[128,640]{1,0:T(8,128)(2,1)S(1)}, u32[]{:S(2)}, u32[]{:S(2)}) collective-permute-start(bf16[128,640]{1,0:T(8,128)(2,1)S(1)} %shard_map.121.refs_4_.refs_0_), channel_id=1, source_target_pairs={{0,4},{1,5},{2,6},{3,7},{4,0},{5,1},{6,2},{7,3},{8,12},{9,13},{10,... | collective-permute-start | bytes 491528 | tf_op jit(solution)/shard_map/ppermute | solution.py:19
  218.2 16.4 %collective-permute-start.39 = (bf16[128,640]{1,0:T(8,128)(2,1)S(1)}, bf16[128,640]{1,0:T(8,128)(2,1)S(1)}, u32[]{:S(2)}, u32[]{:S(2)}) collective-permute-start(bf16[128,640]{1,0:T(8,128)(2,1)S(1)} %shard_map.121.refs_4_.refs_0_), channel_id=1, source_target_pairs={{0,6},{1,7},{2,4},{3,5},{4,2},{5,3},{6,0},{7,1},{8,14},{9,15},{10,... | collective-permute-start | bytes 491528 | tf_op jit(solution)/shard_map/ppermute | solution.py:19
  239.2 29.0 %collective-permute-start.47 = (bf16[128,2048]{1,0:T(8,128)(2,1)S(1)}, bf16[128,2048]{1,0:T(8,128)(2,1)S(1)}, u32[]{:S(2)}, u32[]{:S(2)}) collective-permute-start(bf16[128,2048]{1,0:T(8,128)(2,1)S(1)} %get-tuple-element.149.rest_0_), channel_id=1, source_target_pairs={{0,8},{8,16},{16,24},{1,9},{9,17},{17,25},{2,10},{10,18},{18,26},{... | collective-permute-start | bytes 1572872 | tf_op jit(solution)/shard_map/ppermute | solution.py:24
  243.5 13.5 %collective-permute-start.49 = (bf16[128,640]{1,0:T(8,128)(2,1)S(1)}, bf16[128,640]{1,0:T(8,128)(2,1)S(1)}, u32[]{:S(2)}, u32[]{:S(2)}) collective-permute-start(bf16[128,640]{1,0:T(8,128)(2,1)S(1)} %shard_map.125.refs_4_.refs_0_), channel_id=1, source_target_pairs={{0,4},{1,5},{2,6},{3,7},{4,0},{5,1},{6,2},{7,3},{8,12},{9,13},{10,... | collective-permute-start | bytes 491528 | tf_op jit(solution)/shard_map/ppermute | solution.py:19
  245.3 16.4 %collective-permute-start.50 = (bf16[128,640]{1,0:T(8,128)(2,1)S(1)}, bf16[128,640]{1,0:T(8,128)(2,1)S(1)}, u32[]{:S(2)}, u32[]{:S(2)}) collective-permute-start(bf16[128,640]{1,0:T(8,128)(2,1)S(1)} %shard_map.125.refs_4_.refs_0_), channel_id=1, source_target_pairs={{0,6},{1,7},{2,4},{3,5},{4,2},{5,3},{6,0},{7,1},{8,14},{9,15},{10,... | collective-permute-start | bytes 491528 | tf_op jit(solution)/shard_map/ppermute | solution.py:19
  266.3 29.0 %collective-permute-start.58 = (bf16[128,2048]{1,0:T(8,128)(2,1)S(1)}, bf16[128,2048]{1,0:T(8,128)(2,1)S(1)}, u32[]{:S(2)}, u32[]{:S(2)}) collective-permute-start(bf16[128,2048]{1,0:T(8,128)(2,1)S(1)} %get-tuple-element.155.rest_0_), channel_id=1, source_target_pairs={{0,8},{8,16},{16,24},{1,9},{9,17},{17,25},{2,10},{10,18},{18,26},{... | collective-permute-start | bytes 1572872 | tf_op jit(solution)/shard_map/ppermute | solution.py:24
  270.5 13.5 %collective-permute-start.60 = (bf16[128,640]{1,0:T(8,128)(2,1)S(1)}, bf16[128,640]{1,0:T(8,128)(2,1)S(1)}, u32[]{:S(2)}, u32[]{:S(2)}) collective-permute-start(bf16[128,640]{1,0:T(8,128)(2,1)S(1)} %shard_map.129.refs_4_.refs_0_), channel_id=1, source_target_pairs={{0,4},{1,5},{2,6},{3,7},{4,0},{5,1},{6,2},{7,3},{8,12},{9,13},{10,... | collective-permute-start | bytes 491528 | tf_op jit(solution)/shard_map/ppermute | solution.py:19
  272.4 16.4 %collective-permute-start.61 = (bf16[128,640]{1,0:T(8,128)(2,1)S(1)}, bf16[128,640]{1,0:T(8,128)(2,1)S(1)}, u32[]{:S(2)}, u32[]{:S(2)}) collective-permute-start(bf16[128,640]{1,0:T(8,128)(2,1)S(1)} %shard_map.129.refs_4_.refs_0_), channel_id=1, source_target_pairs={{0,6},{1,7},{2,4},{3,5},{4,2},{5,3},{6,0},{7,1},{8,14},{9,15},{10,... | collective-permute-start | bytes 491528 | tf_op jit(solution)/shard_map/ppermute | solution.py:19
  293.4 29.0 %collective-permute-start.69 = (bf16[128,2048]{1,0:T(8,128)(2,1)S(1)}, bf16[128,2048]{1,0:T(8,128)(2,1)S(1)}, u32[]{:S(2)}, u32[]{:S(2)}) collective-permute-start(bf16[128,2048]{1,0:T(8,128)(2,1)S(1)} %get-tuple-element.161.rest_0_), channel_id=1, source_target_pairs={{0,8},{8,16},{16,24},{1,9},{9,17},{17,25},{2,10},{10,18},{18,26},{... | collective-permute-start | bytes 1572872 | tf_op jit(solution)/shard_map/ppermute | solution.py:24
  297.6 13.5 %collective-permute-start.56 = (bf16[128,640]{1,0:T(8,128)(2,1)S(1)}, bf16[128,640]{1,0:T(8,128)(2,1)S(1)}, u32[]{:S(2)}, u32[]{:S(2)}) collective-permute-start(bf16[128,640]{1,0:T(8,128)(2,1)S(1)} %shard_map.133.refs_4_.refs_0_), channel_id=1, source_target_pairs={{0,4},{1,5},{2,6},{3,7},{4,0},{5,1},{6,2},{7,3},{8,12},{9,13},{10,... | collective-permute-start | bytes 491528 | tf_op jit(solution)/shard_map/ppermute | solution.py:19
  299.5 16.4 %collective-permute-start.57 = (bf16[128,640]{1,0:T(8,128)(2,1)S(1)}, bf16[128,640]{1,0:T(8,128)(2,1)S(1)}, u32[]{:S(2)}, u32[]{:S(2)}) collective-permute-start(bf16[128,640]{1,0:T(8,128)(2,1)S(1)} %shard_map.133.refs_4_.refs_0_), channel_id=1, source_target_pairs={{0,6},{1,7},{2,4},{3,5},{4,2},{5,3},{6,0},{7,1},{8,14},{9,15},{10,... | collective-permute-start | bytes 491528 | tf_op jit(solution)/shard_map/ppermute | solution.py:19
  320.5 29.0 %collective-permute-start.65 = (bf16[128,2048]{1,0:T(8,128)(2,1)S(1)}, bf16[128,2048]{1,0:T(8,128)(2,1)S(1)}, u32[]{:S(2)}, u32[]{:S(2)}) collective-permute-start(bf16[128,2048]{1,0:T(8,128)(2,1)S(1)} %get-tuple-element.167.rest_0_), channel_id=1, source_target_pairs={{0,8},{8,16},{16,24},{1,9},{9,17},{17,25},{2,10},{10,18},{18,26},{... | collective-permute-start | bytes 1572872 | tf_op jit(solution)/shard_map/ppermute | solution.py:24
  326.6 16.4 %collective-permute-start.68 = (bf16[128,640]{1,0:T(8,128)(2,1)S(1)}, bf16[128,640]{1,0:T(8,128)(2,1)S(1)}, u32[]{:S(2)}, u32[]{:S(2)}) collective-permute-start(bf16[128,640]{1,0:T(8,128)(2,1)S(1)} %shard_map.137.refs_4_.refs_0_), channel_id=1, source_target_pairs={{0,6},{1,7},{2,4},{3,5},{4,2},{5,3},{6,0},{7,1},{8,14},{9,15},{10,... | collective-permute-start | bytes 491528 | tf_op jit(solution)/shard_map/ppermute | solution.py:19
  347.6 29.0 %collective-permute-start.76 = (bf16[128,2048]{1,0:T(8,128)(2,1)S(1)}, bf16[128,2048]{1,0:T(8,128)(2,1)S(1)}, u32[]{:S(2)}, u32[]{:S(2)}) collective-permute-start(bf16[128,2048]{1,0:T(8,128)(2,1)S(1)} %get-tuple-element.173.rest_0_), channel_id=1, source_target_pairs={{0,8},{8,16},{16,24},{1,9},{9,17},{17,25},{2,10},{10,18},{18,26},{... | collective-permute-start | bytes 1572872 | tf_op jit(solution)/shard_map/ppermute | solution.py:24
  351.8 13.5 %collective-permute-start.78 = (bf16[128,640]{1,0:T(8,128)(2,1)S(1)}, bf16[128,640]{1,0:T(8,128)(2,1)S(1)}, u32[]{:S(2)}, u32[]{:S(2)}) collective-permute-start(bf16[128,640]{1,0:T(8,128)(2,1)S(1)} %shard_map.141.refs_4_.refs_0_), channel_id=1, source_target_pairs={{0,4},{1,5},{2,6},{3,7},{4,0},{5,1},{6,2},{7,3},{8,12},{9,13},{10,... | collective-permute-start | bytes 491528 | tf_op jit(solution)/shard_map/ppermute | solution.py:19
  353.7 16.4 %collective-permute-start.79 = (bf16[128,640]{1,0:T(8,128)(2,1)S(1)}, bf16[128,640]{1,0:T(8,128)(2,1)S(1)}, u32[]{:S(2)}, u32[]{:S(2)}) collective-permute-start(bf16[128,640]{1,0:T(8,128)(2,1)S(1)} %shard_map.141.refs_4_.refs_0_), channel_id=1, source_target_pairs={{0,6},{1,7},{2,4},{3,5},{4,2},{5,3},{6,0},{7,1},{8,14},{9,15},{10,... | collective-permute-start | bytes 491528 | tf_op jit(solution)/shard_map/ppermute | solution.py:19
  374.7 29.2 %collective-permute-start.87 = (bf16[128,2048]{1,0:T(8,128)(2,1)S(1)}, bf16[128,2048]{1,0:T(8,128)(2,1)S(1)}, u32[]{:S(2)}, u32[]{:S(2)}) collective-permute-start(bf16[128,2048]{1,0:T(8,128)(2,1)S(1)} %get-tuple-element.179.rest_0_), channel_id=1, source_target_pairs={{0,8},{8,16},{16,24},{1,9},{9,17},{17,25},{2,10},{10,18},{18,26},{... | collective-permute-start | bytes 1572872 | tf_op jit(solution)/shard_map/ppermute | solution.py:24
  378.9 13.5 %collective-permute-start.74 = (bf16[128,640]{1,0:T(8,128)(2,1)S(1)}, bf16[128,640]{1,0:T(8,128)(2,1)S(1)}, u32[]{:S(2)}, u32[]{:S(2)}) collective-permute-start(bf16[128,640]{1,0:T(8,128)(2,1)S(1)} %shard_map.145.refs_4_.refs_0_), channel_id=1, source_target_pairs={{0,4},{1,5},{2,6},{3,7},{4,0},{5,1},{6,2},{7,3},{8,12},{9,13},{10,... | collective-permute-start | bytes 491528 | tf_op jit(solution)/shard_map/ppermute | solution.py:19
  380.7 16.4 %collective-permute-start.75 = (bf16[128,640]{1,0:T(8,128)(2,1)S(1)}, bf16[128,640]{1,0:T(8,128)(2,1)S(1)}, u32[]{:S(2)}, u32[]{:S(2)}) collective-permute-start(bf16[128,640]{1,0:T(8,128)(2,1)S(1)} %shard_map.145.refs_4_.refs_0_), channel_id=1, source_target_pairs={{0,6},{1,7},{2,4},{3,5},{4,2},{5,3},{6,0},{7,1},{8,14},{9,15},{10,... | collective-permute-start | bytes 491528 | tf_op jit(solution)/shard_map/ppermute | solution.py:19
  401.7 27.2 %collective-permute-start.83 = (bf16[128,2048]{1,0:T(8,128)(2,1)S(1)}, bf16[128,2048]{1,0:T(8,128)(2,1)S(1)}, u32[]{:S(2)}, u32[]{:S(2)}) collective-permute-start(bf16[128,2048]{1,0:T(8,128)(2,1)S(1)} %get-tuple-element.185.rest_0_), channel_id=1, source_target_pairs={{0,8},{8,16},{16,24},{1,9},{9,17},{17,25},{2,10},{10,18},{18,26},{... | collective-permute-start | bytes 1572872 | tf_op jit(solution)/shard_map/ppermute | solution.py:24
  406.1 13.5 %collective-permute-start.85 = (bf16[128,640]{1,0:T(8,128)(2,1)S(1)}, bf16[128,640]{1,0:T(8,128)(2,1)S(1)}, u32[]{:S(2)}, u32[]{:S(2)}) collective-permute-start(bf16[128,640]{1,0:T(8,128)(2,1)S(1)} %shard_map.149.refs_4_.refs_0_), channel_id=1, source_target_pairs={{0,4},{1,5},{2,6},{3,7},{4,0},{5,1},{6,2},{7,3},{8,12},{9,13},{10,... | collective-permute-start | bytes 491528 | tf_op jit(solution)/shard_map/ppermute | solution.py:19
  408.0 16.4 %collective-permute-start.86 = (bf16[128,640]{1,0:T(8,128)(2,1)S(1)}, bf16[128,640]{1,0:T(8,128)(2,1)S(1)}, u32[]{:S(2)}, u32[]{:S(2)}) collective-permute-start(bf16[128,640]{1,0:T(8,128)(2,1)S(1)} %shard_map.149.refs_4_.refs_0_), channel_id=1, source_target_pairs={{0,6},{1,7},{2,4},{3,5},{4,2},{5,3},{6,0},{7,1},{8,14},{9,15},{10,... | collective-permute-start | bytes 491528 | tf_op jit(solution)/shard_map/ppermute | solution.py:19
  433.2 24.3 %collective-permute-start.97 = (bf16[128,640]{1,0:T(8,128)(2,1)S(1)}, bf16[128,640]{1,0:T(8,128)(2,1)S(1)}, u32[]{:S(2)}, u32[]{:S(2)}) collective-permute-start(bf16[128,640]{1,0:T(8,128)(2,1)S(1)} %shard_map.153.refs_4_.refs_0_), channel_id=1, source_target_pairs={{0,6},{1,7},{2,4},{3,5},{4,2},{5,3},{6,0},{7,1},{8,14},{9,15},{10,... | collective-permute-start | bytes 491528 | tf_op jit(solution)/shard_map/ppermute | solution.py:19
  435.0 22.8 %collective-permute-start.91 = (bf16[128,640]{1,0:T(8,128)(2,1)S(1)}, bf16[128,640]{1,0:T(8,128)(2,1)S(1)}, u32[]{:S(2)}, u32[]{:S(2)}) collective-permute-start(bf16[128,640]{1,0:T(8,128)(2,1)S(1)} %shard_map.157.refs_0_.refs_4_), channel_id=1, source_target_pairs={{0,2},{1,3},{2,0},{3,1},{4,6},{5,7},{6,4},{7,5},{8,10},{9,11},{10,... | collective-permute-start | bytes 491528 | tf_op jit(solution)/shard_map/ppermute | solution.py:19
  436.0 23.0 %collective-permute-start.92 = (bf16[128,640]{1,0:T(8,128)(2,1)S(1)}, bf16[128,640]{1,0:T(8,128)(2,1)S(1)}, u32[]{:S(2)}, u32[]{:S(2)}) collective-permute-start(bf16[128,640]{1,0:T(8,128)(2,1)S(1)} %shard_map.157.refs_0_.refs_4_), channel_id=1, source_target_pairs={{0,4},{1,5},{2,6},{3,7},{4,0},{5,1},{6,2},{7,3},{8,12},{9,13},{10,... | collective-permute-start | bytes 491528 | tf_op jit(solution)/shard_map/ppermute | solution.py:19
  438.4 25.2 %collective-permute-start.93 = (bf16[128,640]{1,0:T(8,128)(2,1)S(1)}, bf16[128,640]{1,0:T(8,128)(2,1)S(1)}, u32[]{:S(2)}, u32[]{:S(2)}) collective-permute-start(bf16[128,640]{1,0:T(8,128)(2,1)S(1)} %shard_map.157.refs_0_.refs_4_), channel_id=1, source_target_pairs={{0,6},{1,7},{2,4},{3,5},{4,2},{5,3},{6,0},{7,1},{8,14},{9,15},{10,... | collective-permute-start | bytes 491528 | tf_op jit(solution)/shard_map/ppermute | solution.py:19
  493.4 19.8 %collective-permute-start.101 = (bf16[128,1024]{1,0:T(8,128)(2,1)S(1)}, bf16[128,1024]{1,0:T(8,128)(2,1)S(1)}, u32[]{:S(2)}, u32[]{:S(2)}) collective-permute-start(bf16[128,1024]{1,0:T(8,128)(2,1)S(1)} %get-tuple-element.205), channel_id=1, source_target_pairs={{0,4},{1,5},{2,6},{3,7},{4,0},{5,1},{6,2},{7,3},{8,12},{9,13},{10,... | collective-permute-start | bytes 786440 | tf_op jit(solution)/shard_map/ppermute | solution.py:19
  495.3 24.8 %collective-permute-start.102 = (bf16[128,1024]{1,0:T(8,128)(2,1)S(1)}, bf16[128,1024]{1,0:T(8,128)(2,1)S(1)}, u32[]{:S(2)}, u32[]{:S(2)}) collective-permute-start(bf16[128,1024]{1,0:T(8,128)(2,1)S(1)} %get-tuple-element.204), channel_id=1, source_target_pairs={{0,6},{1,7},{2,4},{3,5},{4,2},{5,3},{6,0},{7,1},{8,14},{9,15},{10,... | collective-permute-start | bytes 786440 | tf_op jit(solution)/shard_map/ppermute | solution.py:19
  (68 other events, 392.2 us)
